TPU v7x, 32 devices: a whole 2x2x4 slice. The times are simulated.
32 devices in a mesh: rows: 8 (over z, x), cols: 4 (over y, core).
Axes of the slice: x: 2, y: 2, z: 4, core: 2. Of those that a mesh axis runs over, the one named last changes fastest.
Arguments:
- bag_index: int32 [512, 128], P(('rows', 'cols')), may hold values from 0 to 262143, as said below
- bag_length: int32 [512, 4], P(('rows', 'cols')), may hold values from 1 to 32
- emb_tables: float32 [4, 262144, 128], P(None, ('rows', 'cols')), may hold values from -0.6 to 0.6
- dense_feats: float32 [512, 128], P(('rows', 'cols')), may hold values from -6 to 6
- w_dense: float32 [128, 1024], replicated, may hold values from -0.5 to 0.5
- w_pair: float32 [10, 1024], replicated, may hold values from -0.5 to 0.5
- top_bias: float32 [1024], replicated, may hold values from -3 to 3
Outputs:
- pooled: float32 [512, 4, 128], P(('rows', 'cols'))
- top_hidden: float32 [512, 1024], P(('rows', 'cols'))
Inputs may be any that keep to these rules, and one draw needn't show every extreme that they name: `bag_length`: slots at or past a bag's length are ignored, whatever they hold. `bag_index`: device d holds rows d * 8192 to (d + 1) * 8192 - 1 of every table; among the 2048 slots (live or not) of the samples of one device, at most 128 hold rows of any one device, and in every draw some device's rows receive exactly 128 slots from every device.
All inputs are finite; a program needn't handle non-finite values.
Results may differ from a plain program's by a relative error of at most 0.0001.
Values sent between devices are 32-bit elements; how exact they have to be, the bound alone decides.
A program may use at most 128 MiB of HBM per device.

v0:
```python
import jax
import jax.numpy as jnp
from jax import lax
from jax.sharding import PartitionSpec as P

NT = 4
L = 32


def interact(dense_feats, pooled, w_dense, w_pair, top_bias):
    feats = [dense_feats] + [pooled[:, t, :] for t in range(NT)]
    pair_list = []
    for first in range(NT + 1):
        for second in range(first + 1, NT + 1):
            pair_list.append(jnp.sum(feats[first] * feats[second], axis=-1))
    pair_dots = jnp.stack(pair_list, axis=1)
    hidden = jnp.dot(
        dense_feats, w_dense, precision=lax.Precision.HIGHEST, preferred_element_type=jnp.float32
    )
    hidden = hidden + jnp.dot(
        pair_dots, w_pair, precision=lax.Precision.HIGHEST, preferred_element_type=jnp.float32
    )
    return jnp.maximum(hidden + top_bias, 0.0)


def shards(bag_index, bag_length, emb_tables, dense_feats, w_dense, w_pair, top_bias):
    samples = bag_index.shape[0]
    local_rows = emb_tables.shape[1]
    width = emb_tables.shape[2]
    position = jnp.arange(L, dtype=jnp.int32)
    devices = lax.axis_size("rows") * lax.axis_size("cols")
    slots = samples * NT * L
    capacity = 2 * slots // devices
    flat_ids = bag_index.reshape(slots)
    target = flat_ids // local_rows
    slot_iota = jnp.arange(slots, dtype=jnp.int32)
    table_of = slot_iota % (NT * L) // L
    code = table_of * local_rows + flat_ids - target * local_rows
    earlier = (slot_iota[None, :] < slot_iota[:, None]) & (target[None, :] == target[:, None])
    rank = jnp.sum(earlier.astype(jnp.int32), axis=1)
    owner_hot = (target[:, None] == jnp.arange(devices, dtype=jnp.int32)[None, :]).astype(
        jnp.float32
    )
    rank_hot = (rank[:, None] == jnp.arange(capacity, dtype=jnp.int32)[None, :]).astype(jnp.float32)
    weighted = owner_hot * code.astype(jnp.float32)[:, None]
    outbox = jnp.einsum(
        "sd,sc->dc",
        weighted,
        rank_hot,
        precision=lax.Precision.HIGHEST,
        preferred_element_type=jnp.float32,
    )
    outbox = outbox.astype(jnp.int32)
    flat_table = emb_tables.reshape(NT * local_rows, width)
    found = jnp.take(
        flat_table,
        lax.all_to_all(outbox, ("rows", "cols"), split_axis=0, concat_axis=0, tiled=True),
        axis=0,
    )
    fetched = lax.all_to_all(found, ("rows", "cols"), split_axis=0, concat_axis=0, tiled=True)
    place = target * capacity + rank
    selector = (place[:, None] == jnp.arange(devices * capacity, dtype=jnp.int32)[None, :]).astype(
        jnp.float32
    )
    picked = jnp.dot(
        selector,
        fetched.reshape(devices * capacity, width),
        precision=lax.Precision.HIGHEST,
        preferred_element_type=jnp.float32,
    )
    picked = picked.reshape(samples, NT, L, width)
    live = position[None, None, :] < bag_length[:, :, None]
    pooled = jnp.sum(jnp.where(live[:, :, :, None], picked, 0.0), axis=2)
    return (pooled, interact(dense_feats, pooled, w_dense, w_pair, top_bias))


def solution(mesh):
    in_specs = (
        P(("rows", "cols"), None),
        P(("rows", "cols"), None),
        P(None, ("rows", "cols"), None),
        P(("rows", "cols"), None),
        P(),
        P(),
        P(),
    )
    out_specs = (P(("rows", "cols"), None, None), P(("rows", "cols"), None))
    return jax.shard_map(shards, mesh=mesh, in_specs=in_specs, out_specs=out_specs, check_vma=False)
```

profile of v0, /device:TPU:0, one launch (start us, length us, event | category | flops | bytes accessed | tf_op | source)
XLA Modules:
  0.0 108.5 jit_solution(8356318084988157493)
XLA Ops:
  0.6 0.0 copy-start
  0.6 0.8 fusion.29
  1.4 4.6 %convert_reduce_fusion = s32[2048]{0:T(1024)S(1)} fusion(s32[2048]{0:T(1024)S(1)} %get-tuple-element.17), kind=kLoop, calls=%fused_computation.5 | loop fusion | flops 20969472 | bytes 16384 | tf_op jit(solution)/shard_map/reduce_sum | solution.py:40
  6.0 1.8 %convolution_convert_fusion = s32[32,128]{1,0:T(8,128)S(1)} fusion(s32[2048]{0:T(1024)S(1)} %convert_reduce_fusion, f32[2048]{0:T(1024)S(1)} %get-tuple-element.16, s32[2048]{0:T(1024)S(1)} %get-tuple-element.17), kind=kOutput, calls=%fused_computation.13 | convolution fusion | flops 101060608 | bytes 40960 | tf_op jit(solution)/shard_map/sd,sc->dc/dot_general | solution.py:46
  7.9 14.3 %all_to_all.20 = s32[32,1,128]{2,1,0:T(1,128)S(1)} all-to-all(s32[32,1,128]{2,1,0:T(1,128)S(1)} %bitcast.76), channel_id=1, replica_groups=mesh['rows'=8,'cols'=4] {'rows','cols'}, dimensions={0} | all-to-all | bytes 32768 | tf_op jit(solution)/shard_map/all_to_all | solution.py:57
  22.2 16.5 %gather_fusion = f32[4096,128]{1,0:T(8,128)S(1)} fusion(f32[32768,128]{1,0:T(8,128)} %bitcast.67, s32[4096]{0:T(1024)S(1)} %fusion.23), kind=kCustom, calls=%fused_computation | custom fusion | bytes 4210688 | tf_op jit(solution)/shard_map/jit(_take)/gather | solution.py:55
  38.7 0.0 copy-start.3
  38.7 0.0 copy-start.6
  38.8 0.0 copy-start.2
  38.8 1.7 %broadcast_select_fusion = f32[32,128,128]{2,1,0:T(8,128)} fusion(f32[32,128,128]{2,1,0:T(8,128)S(1)} %bitcast.68, pred[32,128]{1,0:T(8,128)(4,1)S(1)} %compare_and_fusion), kind=kLoop, calls=%fused_computation.14 | loop fusion | flops 524288 | bytes 4198400 | tf_op jit(solution)/shard_map/jit(_take)/select_n | solution.py:55
  40.5 2.9 %all-to-all-start.1 = ((f32[32,128,128]{2,1,0:T(8,128)}), f32[32,128,128]{2,1,0:T(8,128)S(1)}, u32[]{:S(2)}, u32[]{:S(2)}) async-start(f32[32,128,128]{2,1,0:T(8,128)} %broadcast_select_fusion), calls=%async_computation.1 | async-start | bytes 4194304 | tf_op jit(solution)/shard_map/all_to_all | solution.py:60
  43.4 0.1 reduce_sum.111
  43.5 0.0 copy-done.3
  43.5 0.1 reshape.192
  43.6 0.0 copy-done.6
  43.6 0.1 copy.18
  43.7 0.1 iota_compare_fusion.6
  43.8 0.0 copy-done
  43.8 0.0 copy-done.2
  43.9 0.4 fusion.39
  44.2 47.7 %all-to-all-done.1 = f32[32,128,128]{2,1,0:T(8,128)S(1)} async-done(((f32[32,128,128]{2,1,0:T(8,128)}), f32[32,128,128]{2,1,0:T(8,128)S(1)}, u32[]{:S(2)}, u32[]{:S(2)}) %all-to-all-start.1) | async-done | bytes 2097184 | tf_op jit(solution)/shard_map/all_to_all | solution.py:60
  91.9 0.0 copy-start.1
  91.9 0.0 copy-start.5
  91.9 15.3 %fusion.8 = f32[16,4,128]{2,1,0:T(4,128)S(1)} fusion(f32[4096,128,1,1]{1,0,3,2:T(8,128)S(1)} %bitcast.69, s32[16,4,32]{2,1,0:T(4,128)S(1)} %fusion.20, pred[16,4,32]{2,1,0:T(4,128)(4,1)S(1)} %iota_compare_fusion.6), kind=kOutput, calls=%fused_computation.9 | convolution fusion | flops 12893806592 | bytes 2140160 | tf_op jit(solution)/shard_map/dot_general | solution.py:65
  107.3 0.0 copy-start.4
  107.3 0.3 multiply_reduce_fusion
  107.6 0.0 copy-done.1
  107.6 0.0 copy-done.5
  107.6 0.9 fusion.12
  108.5 0.0 copy-done.4
  (5 shorter events, 0.1 us)
Async XLA Ops:
  0.6 43.2 %copy-start = (f32[128,1024]{1,0:T(8,128)S(1)}, f32[128,1024]{1,0:T(8,128)}, u32[]{:S(2)}) copy-start(f32[128,1024]{1,0:T(8,128)} %param.11) | copy-start | bytes 1572868
  38.7 4.8 %copy-start.3 = (s32[16,128]{1,0:T(8,128)S(1)}, s32[16,128]{1,0:T(8,128)}, u32[]{:S(2)}) copy-start(s32[16,128]{1,0:T(8,128)} %param.7) | copy-start | bytes 24580
  38.7 4.9 %copy-start.6 = (s32[16,4]{0,1:T(4,128)S(1)}, s32[16,4]{0,1:T(4,128)}, u32[]{:S(2)}) copy-start(s32[16,4]{0,1:T(4,128)} %param.8) | copy-start | bytes 772
  38.8 5.1 %copy-start.2 = (f32[16,128]{1,0:T(8,128)S(1)}, f32[16,128]{1,0:T(8,128)}, u32[]{:S(2)}) copy-start(f32[16,128]{1,0:T(8,128)} %param.10) | copy-start | bytes 24580
  40.5 51.4 %all-to-all-start.1 = ((f32[32,128,128]{2,1,0:T(8,128)}), f32[32,128,128]{2,1,0:T(8,128)S(1)}, u32[]{:S(2)}, u32[]{:S(2)}) async-start(f32[32,128,128]{2,1,0:T(8,128)} %broadcast_select_fusion), calls=%async_computation.1 | async-start | bytes 4194304 | tf_op jit(solution)/shard_map/all_to_all | solution.py:60
  91.9 15.7 %copy-start.1 = (f32[10,1024]{1,0:T(8,128)S(1)}, f32[10,1024]{1,0:T(8,128)}, u32[]{:S(2)}) copy-start(f32[10,1024]{1,0:T(8,128)} %param.12) | copy-start | bytes 122884
  91.9 15.7 %copy-start.5 = (f32[1024]{0:T(1024)S(1)}, f32[1024]{0:T(1024)}, u32[]{:S(2)}) copy-start(f32[1024]{0:T(1024)} %param.13) | copy-start | bytes 12292
  107.3 1.3 %copy-start.4 = (f32[16,4,128]{2,1,0:T(4,128)}, f32[16,4,128]{2,1,0:T(4,128)S(1)}, u32[]{:S(2)}) copy-start(f32[16,4,128]{2,1,0:T(4,128)S(1)} %fusion.8) | copy-start | bytes 98308
where the time goes:
time: 109 us
  waiting for transfers between devices  47.7 us (44%)
  matrix products  18.4 us (17%)
  local copies, waits for them, and re-layouts  16.9 us (16%)
  blocking collectives  14.3 us (13%)
  other arithmetic  7.52 us (7%)
  starting transfers between devices  2.91 us (3%)
    all_to_all x1, waiting for transfers between devices, shards(): lax.all_to_all(found, ('rows', 'cols'), split_axis=0, concat_axis=0, tile...  47.7 us
    gather x1, local copies, waits for them, and re-layouts, shards(): jnp.take(flat_table, lax.all_to_all(outbox, ('rows', 'cols'), split_axis=...  16.5 us
    dot_general x1, matrix products, shards(): jnp.dot(selector, fetched.reshape(devices * capacity, width), precision=l...  15.3 us
    all_to_all x1, blocking collectives, shards(): lax.all_to_all(outbox, ('rows', 'cols'), split_axis=0, concat_axis=0, til...  14.3 us
    reduce_sum x1, other arithmetic, shards(): rank = jnp.sum(earlier.astype(jnp.int32), axis=1)  4.6 us
    all_to_all x1, starting transfers between devices, shards(): lax.all_to_all(found, ('rows', 'cols'), split_axis=0, concat_axis=0, tile...  2.91 us
  transfers between devices with their start and end apart: 1, of which 1 were waited for; matrix products, arithmetic and copies ran while one was open for 1% of the time, Pallas kernels for 0%

commit v1 on v0

v1 whole, which is shorter than its diff:
```python
import functools

import jax
import jax.numpy as jnp
from jax import lax
from jax.experimental import pallas as pl
from jax.experimental.pallas import tpu as pltpu
from jax.sharding import PartitionSpec as P

MESH = pl.DeviceIdType.MESH
F32 = jnp.float32
BF16 = jnp.bfloat16
LAG = 3
LAG_Z = 4
CHUNKS = 8


def kernel(
    dims,
    index_ref,
    length_ref,
    table_hbm,
    dense_ref,
    wd_hbm,
    wp_ref,
    bias_ref,
    pooled_ref,
    hidden_ref,
    table,
    wd,
    hidden,
    outbox,
    inbox,
    ids,
    rows_buf,
    core_out,
    core_in,
    keep,
    plane_out,
    plane_in,
    z_out,
    z_in,
    table_sem,
    wd_sem,
    box_send,
    box_recv,
    ids_sem,
    core_send,
    core_recv,
    plane_send,
    plane_recv,
    z_send,
    z_recv,
):
    nr, nc, nx, local_rows, nt, slots_bag, cap = dims
    n = nr * nc
    ny = nc // 2
    np_ = nx * ny
    nz = nr // nx
    groups = nz * np_
    samples, lanes = index_ref.shape
    width = table.shape[1]
    bags = samples * nt
    total_rows = nt * local_rows
    r = lax.axis_index("rows")
    c = lax.axis_index("cols")
    me = r * nc + c
    z, x, y, k = r // nx, r % nx, c // 2, c % 2
    p = x * ny + y

    def at(d):
        return {"rows": d // nc, "cols": d % nc}

    def place(zz, pp, kk):
        return zz * nx + pp // ny, (pp % ny) * 2 + kk

    def flat(zz, pp, kk):
        rr, cc = place(zz, pp, kk)
        return rr * nc + cc

    barrier = pltpu.get_barrier_semaphore()

    def greet(i, carry):
        d = (me + i) % n
        pl.semaphore_signal(barrier, inc=1, device_id=at(d), device_id_type=MESH)
        return carry

    lax.fori_loop(1, n, greet, 0)

    part = total_rows // CHUNKS
    table_copies = [
        pltpu.make_async_copy(
            table_hbm.at[pl.ds(i * part, part)], table.at[pl.ds(i * part, part)], table_sem.at[i]
        )
        for i in range(CHUNKS)
    ]
    wd_copy = pltpu.make_async_copy(wd_hbm, wd, wd_sem)
    for copy in table_copies:
        copy.start()
    wd_copy.start()

    idx = index_ref[...]
    lane = lax.broadcasted_iota(jnp.int32, (samples, lanes), 1)
    table_of = lane // slots_bag
    length = jnp.zeros((samples, lanes), jnp.int32)
    for t in range(nt):
        length = jnp.where(table_of == t, length_ref[:, t : t + 1], length)
    live = lane - table_of * slots_bag < length
    if local_rows & (local_rows - 1) == 0:
        owner = lax.shift_right_logical(idx, jnp.full_like(idx, local_rows.bit_length() - 1))
    else:
        owner = idx // local_rows
    row = table_of * local_rows + idx - owner * local_rows
    bag = table_of * samples + lax.broadcasted_iota(jnp.int32, (samples, lanes), 0)
    owner = jnp.where(live, owner, -1)
    pieces = []
    shift = 0
    while shift == 0 or (total_rows - 1) >> shift:
        pieces.append((row // (1 << shift)) % 256)
        shift += 8
    n_row = len(pieces)
    shift = 0
    while shift == 0 or bags >> shift:
        pieces.append(((bag + 1) // (1 << shift)) % 256)
        shift += 8
    pieces = [v.astype(F32) for v in pieces]
    dev_iota = lax.broadcasted_iota(jnp.int32, (n, lanes), 0)
    before = (
        lax.broadcasted_iota(jnp.int32, (lanes, lanes), 0)
        < lax.broadcasted_iota(jnp.int32, (lanes, lanes), 1)
    )
    before = jnp.where(before, 1.0, 0.0).astype(BF16)
    hots = [
        jnp.where(owner[b : b + 1, :] == dev_iota, 1.0, 0.0).astype(F32) for b in range(samples)
    ]
    prefix = jnp.dot(
        jnp.concatenate([h.astype(BF16) for h in hots], axis=0), before, preferred_element_type=F32
    )
    base = jnp.zeros((n, 1), F32)
    box = jnp.zeros((len(pieces) * n, cap), F32)
    cap_iota = lax.broadcasted_iota(jnp.int32, (cap, lanes), 0)
    for b in range(samples):
        hot = hots[b]
        rank = jnp.sum(hot * (prefix[b * n : (b + 1) * n, :] + base), axis=0, keepdims=True)
        base = base + jnp.sum(hot, axis=1, keepdims=True)
        spot = jnp.where(rank.astype(jnp.int32) == cap_iota, 1.0, 0.0).astype(BF16)
        coded = jnp.concatenate([hot * v[b : b + 1, :] for v in pieces], axis=0).astype(BF16)
        box = box + lax.dot_general(
            coded, spot, (((1,), (1,)), ((), ())), preferred_element_type=F32
        )
    box_row = jnp.zeros((n, cap), jnp.int32)
    box_bag = jnp.full((n, cap), -1, jnp.int32)
    for i in range(len(pieces)):
        piece = box[i * n : (i + 1) * n, :].astype(jnp.int32)
        if i < n_row:
            box_row = box_row + piece * (1 << (8 * i))
        else:
            box_bag = box_bag + piece * (1 << (8 * (i - n_row)))
    for d in range(n):
        outbox[d, 0:1, :] = box_row[d : d + 1, :]
        outbox[d, 1:2, :] = box_bag[d : d + 1, :]
    inbox[me] = outbox[me]

    pl.semaphore_wait(barrier, n - 1)

    def box_copy(d, source):
        return pltpu.make_async_remote_copy(
            src_ref=outbox.at[d],
            dst_ref=inbox.at[source],
            send_sem=box_send.at[d],
            recv_sem=box_recv.at[source],
            device_id=at(d),
            device_id_type=MESH,
        )

    def send_box(i, carry):
        box_copy((me + i) % n, me).start()
        return carry

    lax.fori_loop(1, n, send_box, 0)

    wd_copy.wait()
    hidden[...] = (
        jnp.dot(
            dense_ref[...], wd[...], precision=lax.Precision.HIGHEST, preferred_element_type=F32
        )
        + bias_ref[...]
    )

    def ids_copy(d):
        return pltpu.make_async_copy(inbox.at[d], ids.at[d], ids_sem.at[d])

    ids_copy(me).start()

    def take_box(i, carry):
        d = (me + n - i) % n
        box_copy((me + i) % n, d).wait_recv()
        ids_copy(d).start()
        return carry

    lax.fori_loop(1, n, take_box, 0)
    for d in range(n):
        ids_copy(d).wait()
    for copy in table_copies:
        copy.wait()

    bag_iota = lax.broadcasted_iota(jnp.int32, (bags, cap), 0)

    def inside(at_row):
        if total_rows & (total_rows - 1) == 0:
            return at_row & (total_rows - 1)
        return jnp.clip(at_row, 0, total_rows - 1)

    def fetch(d, slot):
        for i in range(cap):
            rows_buf[slot, i : i + 1, :] = table[pl.ds(inside(ids[d, 0, i]), 1), :]

    def pool(d, slot):
        found = rows_buf[slot]
        high = found.astype(BF16)
        low = (found - high.astype(F32)).astype(BF16)
        select = jnp.where(inbox[d, 1:2, :] == bag_iota, 1.0, 0.0).astype(BF16)
        both = jnp.dot(select, jnp.concatenate([high, low], axis=1), preferred_element_type=F32)
        return both[:, :width] + both[:, width:]

    def target(j):
        return (z + 1 + j // np_) % nz, (p + 1 + j % np_) % np_

    def core_copy(g):
        return pltpu.make_async_remote_copy(
            src_ref=core_out.at[g],
            dst_ref=core_in.at[g],
            send_sem=core_send.at[g],
            recv_sem=core_recv.at[g],
            device_id={"rows": r, "cols": y * 2 + 1 - k},
            device_id_type=MESH,
        )

    def plane_copy(zz, pp, source):
        rr, cc = place(z, pp, k)
        return pltpu.make_async_remote_copy(
            src_ref=plane_out.at[zz * np_ + pp],
            dst_ref=plane_in.at[zz * np_ + source],
            send_sem=plane_send.at[zz * np_ + pp],
            recv_sem=plane_recv.at[zz * np_ + source],
            device_id={"rows": rr, "cols": cc},
            device_id_type=MESH,
        )

    def z_copy(zz, source):
        rr, cc = place(zz, p, k)
        return pltpu.make_async_remote_copy(
            src_ref=z_out.at[zz],
            dst_ref=z_in.at[source],
            send_sem=z_send.at[zz],
            recv_sem=z_recv.at[source],
            device_id={"rows": rr, "cols": cc},
            device_id_type=MESH,
        )

    def step(it, carry):
        @pl.when(it < groups)
        def _():
            zz, pp = target(it)
            g = zz * np_ + pp
            mate = flat(zz, pp, 1 - k)
            own = flat(zz, pp, k)
            fetch(mate, 0)
            core_out[g] = pool(mate, 0)
            fetch(own, 1)
            keep[g] = pool(own, 1)
            core_copy(g).start()

        j = it - LAG

        @pl.when((j >= 0) & (j < groups))
        def _():
            zz, pp = target(j)
            g = zz * np_ + pp
            core_copy(g).wait_recv()
            summed = core_in[g] + keep[g]

            @pl.when(j % np_ == np_ - 1)
            def _():
                plane_in[g] = summed

            @pl.when(j % np_ < np_ - 1)
            def _():
                plane_out[g] = summed
                plane_copy(zz, pp, p).start()

        h = it - LAG - LAG_Z

        @pl.when((h >= 0) & (h % np_ == np_ - 1))
        def _():
            zi = h // np_
            zz = (z + 1 + zi) % nz
            summed = plane_in[zz * np_ + p]
            for i in range(1, np_):
                other = (p + i) % np_
                plane_copy(zz, other, other).wait_recv()
                summed = summed + plane_in[zz * np_ + other]

            @pl.when(zi < nz - 1)
            def _():
                z_out[zz] = summed
                z_copy(zz, z).start()

            @pl.when(zi == nz - 1)
            def _():
                z_in[z] = summed

        return carry

    lax.fori_loop(0, groups + LAG + LAG_Z, step, 0)

    pooled = z_in[z]
    for i in range(1, nz):
        other = (z + i) % nz
        z_copy(other, other).wait_recv()
        pooled = pooled + z_in[other]

    feats = [dense_ref[...]]
    for t in range(nt):
        feats.append(pooled[t * samples : (t + 1) * samples, :])
        pooled_ref[:, t, :] = feats[-1]
    total = hidden[...]
    pair = 0
    for first in range(nt + 1):
        for second in range(first + 1, nt + 1):
            dots = jnp.sum(feats[first] * feats[second], axis=-1, keepdims=True)
            total = total + dots * wp_ref[pair : pair + 1, :]
            pair += 1
    hidden_ref[...] = jnp.maximum(total, 0.0)

    def drain_box(i, carry):
        box_copy((me + i) % n, me).wait_send()
        return carry

    lax.fori_loop(1, n, drain_box, 0)

    def drain(j, carry):
        zz, pp = target(j)
        core_copy(zz * np_ + pp).wait_send()

        @pl.when(j % np_ < np_ - 1)
        def _():
            plane_copy(zz, pp, p).wait_send()

        return carry

    lax.fori_loop(0, groups, drain, 0)
    for i in range(1, nz):
        z_copy((z + i) % nz, z).wait_send()


def shards(nr, nc, bag_index, bag_length, emb_tables, dense_feats, w_dense, w_pair, top_bias):
    samples, lanes = bag_index.shape
    nt, local_rows, width = emb_tables.shape
    n = nr * nc
    slots = samples * lanes
    cap = 2 * slots // n
    bags = samples * nt
    units = w_dense.shape[1]
    nx = 2 if nr % 2 == 0 else 1
    groups = n // 2
    nz = nr // nx
    dims = (nr, nc, nx, local_rows, nt, lanes // nt, cap)
    vmem = pl.BlockSpec(memory_space=pltpu.VMEM)
    anyw = pl.BlockSpec(memory_space=pl.ANY)
    blocks = lambda m: pltpu.VMEM((m, bags, width), F32)
    dma = pltpu.SemaphoreType.DMA
    pooled, hidden = pl.pallas_call(
        functools.partial(kernel, dims),
        out_shape=(
            jax.ShapeDtypeStruct((samples, nt, width), F32),
            jax.ShapeDtypeStruct((samples, units), F32),
        ),
        in_specs=[vmem, vmem, anyw, vmem, anyw, vmem, vmem],
        out_specs=(vmem, vmem),
        scratch_shapes=[
            pltpu.VMEM((nt * local_rows, width), F32),
            pltpu.VMEM(w_dense.shape, F32),
            pltpu.VMEM((samples, units), F32),
            pltpu.VMEM((n, 2, cap), jnp.int32),
            pltpu.VMEM((n, 2, cap), jnp.int32),
            pltpu.SMEM((n, 2, cap), jnp.int32),
            pltpu.VMEM((2, cap, width), F32),
            blocks(groups),
            blocks(groups),
            blocks(groups),
            blocks(groups),
            blocks(groups),
            blocks(nz),
            blocks(nz),
            dma((CHUNKS,)),
            dma,
            dma((n,)),
            dma((n,)),
            dma((n,)),
            dma((groups,)),
            dma((groups,)),
            dma((groups,)),
            dma((groups,)),
            dma((nz,)),
            dma((nz,)),
        ],
        compiler_params=pltpu.CompilerParams(
            collective_id=0, has_side_effects=True, vmem_limit_bytes=60 * 1024 * 1024
        ),
    )(
        bag_index,
        bag_length,
        emb_tables.reshape(nt * local_rows, width),
        dense_feats,
        w_dense,
        w_pair,
        top_bias.reshape(1, units),
    )
    return pooled, hidden


def solution(mesh):
    nr, nc = mesh.shape["rows"], mesh.shape["cols"]
    in_specs = (
        P(("rows", "cols"), None),
        P(("rows", "cols"), None),
        P(None, ("rows", "cols"), None),
        P(("rows", "cols"), None),
        P(),
        P(),
        P(),
    )
    out_specs = (P(("rows", "cols"), None, None), P(("rows", "cols"), None))
    return jax.shard_map(
        functools.partial(shards, nr, nc),
        mesh=mesh,
        in_specs=in_specs,
        out_specs=out_specs,
        check_vma=False,
    )
```

time: 109 us -> 34 us (0.31)
  waiting for transfers between devices: 47.7 us -> 0 us
  Pallas kernels: 0 us -> 28.9 us
  matrix products: 18.4 us -> 0 us
  blocking collectives: 14.3 us -> 0 us
  local copies, waits for them, and re-layouts: 16.9 us -> 4.2 us
  other arithmetic: 7.52 us -> 0 us
  starting transfers between devices: 2.91 us -> 0 us
    all_to_all x1 -> x0, waiting for transfers between devices: 47.7 us -> none  [shards(): lax.all_to_all(found, ('rows', 'cols'), split_axis=0, concat_axis=0, tile...]
    pallas_call x0 -> x1, Pallas kernels: none -> 28.9 us  [shards(): pl.pallas_call(functools.partial(kernel, dims), out_shape=(jax.ShapeDtype...]
    dot_general x4 -> x0, matrix products: 18.4 us -> none  [the longest x1 15.3 us: shards(): jnp.dot(selector, fetched.reshape(devices * capacity, width), precision=l...]
    gather x1 -> x0, local copies, waits for them, and re-layouts: 16.5 us -> none  [shards(): jnp.take(flat_table, lax.all_to_all(outbox, ('rows', 'cols'), split_axis=...]
    all_to_all x1 -> x0, blocking collectives: 14.3 us -> none  [shards(): lax.all_to_all(outbox, ('rows', 'cols'), split_axis=0, concat_axis=0, til...]
    reduce_sum x2 -> x0, other arithmetic: 4.86 us -> none  [the longest x1 4.6 us: shards(): rank = jnp.sum(earlier.astype(jnp.int32), axis=1)]
    unnamed x15 -> x3, local copies, waits for them, and re-layouts: 0.12 us -> 4.2 us
    all_to_all x1 -> x0, starting transfers between devices: 2.91 us -> none  [shards(): lax.all_to_all(found, ('rows', 'cols'), split_axis=0, concat_axis=0, tile...]
  transfers between devices with their start and end apart: 1 -> 0, of which waited for: 1 -> 0; matrix products, arithmetic and copies ran while one was open for 1% -> 0% of each run, Pallas kernels for 0% -> 0%
where the time goes in v1:
time: 34 us; the launch traced here: 33.7 us
  Pallas kernels  28.9 us (85%)
  local copies, waits for them, and re-layouts  4.2 us (12%)
  between operations  0.64 us (2%)
    pallas_call x1, Pallas kernels, shards(): pl.pallas_call(functools.partial(kernel, dims), out_shape=(jax.ShapeDtype...  28.9 us
    unnamed x3, local copies, waits for them, and re-layouts  4.2 us

profile of v1, /device:TPU:0, one launch (start us, length us, event | category | flops | bytes accessed | tf_op | source)
XLA Modules:
  0.0 33.7 jit_solution(13626603231987745030)
XLA Ops:
  0.6 1.4 %copy.9.length_ref = s32[16,4]{1,0:T(8,128)} copy(s32[16,4]{0,1:T(4,128)} %param.8) | data formatting | bytes 512 | tf_op args[1]
  2.0 28.9 %shard_map.86 = (f32[16,4,128]{2,1,0:T(4,128)}, f32[16,1024]{1,0:T(8,128)}) custom-call(s32[16,128]{1,0:T(8,128)} %index_ref.1, s32[16,4]{1,0:T(8,128)} %copy.9.length_ref, f32[32768,128]{1,0:T(8,128)} %bitcast.2, f32[16,128]{1,0:T(8,128)} %dense_ref.1, f32[128,1024]{1,0:T(8,128)} %wd_hbm.1, f32[10,1024]{1,0:T(8,128)} %wp_ref.1, f32[1,1024]{1,0:T(1,128)} %bitcast.3), custom_call_target="tpu_custom_call" | custom-call | tf_op jit(solution)/shard_map/pallas_call | solution.py:373
  30.9 1.4 %copy.12 = f32[16,4,128]{2,1,0:T(4,128)} copy(f32[16,4,128]{2,1,0:T(4,128)} %get-tuple-element.4) | data formatting | bytes 65536
  32.3 1.5 %copy.13 = f32[16,1024]{1,0:T(8,128)} copy(f32[16,1024]{1,0:T(8,128)} %get-tuple-element.5) | data formatting | bytes 131072
